TPU v7x, 32 devices: a whole 2x2x4 slice. The times are simulated.
32 devices in a mesh: grp: 2 (over x), gx: 8 (over z, y), gz: 2 (over core).
Axes of the slice: x: 2, y: 2, z: 4, core: 2. Of those that a mesh axis runs over, the one named last changes fastest.
Arguments:
- electric: float32 [512, 8192], P(('grp', 'gx'), 'gz'), parts along dimension 0, may hold values from -6 to 6
- magnetic_x: float32 [512, 8192], P(('grp', 'gx'), 'gz'), parts along dimension 0, may hold values from -6 to 6
- magnetic_z: float32 [512, 8192], P(('grp', 'gx'), 'gz'), parts along dimension 0, may hold values from -6 to 6
- index_map: int32 [4, 64, 8192], P(None, None, 'gz'), may hold values from 0 to 3
- period_seq: int32 [10], P('grp'), parts along dimension 0, may hold values from 0 to 3
- eps_table: float32 [4], replicated, may hold values from 1 to 12.25
- shifts: int32 [8], P('grp'), parts along dimension 0, may hold values from 0 to 4, as said below
Outputs:
- electric_out: float32 [512, 8192], P(('grp', 'gx'), 'gz'), parts along dimension 0
- magnetic_x_out: float32 [512, 8192], P(('grp', 'gx'), 'gz'), parts along dimension 0
- magnetic_z_out: float32 [512, 8192], P(('grp', 'gx'), 'gz'), parts along dimension 0
There are 2 independent parts, one for each index of `grp`. A program takes and returns all parts, laid end to end along the dimension named above; an argument that names none is the same for every part. Nothing has to cross between parts.
Inputs may be any that keep to these rules, and one draw needn't show every extreme that they name: `shifts`: every entry is at most 4, and some entry equals 4.
All inputs are finite; a program needn't handle non-finite values.
Results may differ from a plain program's by a relative error of at most 0.00016.
Values sent between devices are 32-bit elements; how exact they have to be, the bound alone decides.
No kernel may reach another device: no remote copies, remote signals or barrier semaphores. Data moves between devices by JAX's collectives and lax.ppermute only.
A program may use at most 64 MiB of HBM per device.

v0:
```python
import jax
import jax.numpy as jnp
from jax import lax
from jax.sharding import PartitionSpec as P

ITERS = 4
SMAX = 4


courant = 0.6


def with_halo(block, sides, width):
    for axis, dim in sides:
        count = lax.axis_size(axis)
        forward = [(i, i + 1) for i in range(count - 1)]
        backward = [(target, source) for source, target in forward]
        low = lax.ppermute(
            lax.slice_in_dim(block, block.shape[dim] - width, None, axis=dim), axis, forward
        )
        high = lax.ppermute(lax.slice_in_dim(block, 0, width, axis=dim), axis, backward)
        block = jnp.concatenate([low, block, high], axis=dim)
    return block


def passed_along(block, axis, distance):
    devices = range(lax.axis_size(axis))
    route = [(i - distance, i) for i in devices if i - distance in devices]
    return lax.ppermute(block, axis, route)


def material(columns, profile, period_seq, inverse):
    span = profile.shape[1]
    period = columns // span
    phase = columns % span
    picked = period[:, None] == jnp.arange(period_seq.shape[0], dtype=jnp.int32)[None, :]
    design = jnp.sum(jnp.where(picked, period_seq[None, :], 0), axis=1)
    rows_all = profile.shape[0] * span
    row_id = design * span + phase
    onehot = (row_id[:, None] == jnp.arange(rows_all, dtype=jnp.int32)[None, :]).astype(jnp.float32)
    table = profile.reshape(rows_all, profile.shape[2]).astype(jnp.float32)
    levels = jnp.dot(onehot, table, precision=lax.Precision.HIGHEST)
    result = jnp.zeros_like(levels)
    for level in range(inverse.shape[0]):
        result = result + jnp.where(levels == level, inverse[level], 0.0)
    return result


def advance(
    extended,
    profile,
    period_seq,
    inverse,
    shifts,
    first,
    count,
    x_start,
    z_start,
    total_x,
    total_z,
    offset,
):
    width = extended.shape[1]
    depth = extended.shape[2]
    tail = jnp.zeros((3, SMAX, depth), extended.dtype)
    columns = x_start + jnp.arange(width, dtype=jnp.int32)
    layers = z_start + jnp.arange(depth, dtype=jnp.int32)
    inside_x = (columns >= 0) & (columns < total_x)
    inside_z = (layers >= 0) & (layers < total_z)
    inside = (inside_x[:, None] & inside_z[None, :]).astype(jnp.float32)
    zero_col = jnp.zeros((width, 1), jnp.float32)
    zero_row = jnp.zeros((1, depth), jnp.float32)
    for step in range(first, first + count):
        moved = shifts[step]
        offset = offset + moved
        extended = lax.dynamic_slice_in_dim(
            jnp.concatenate([extended, tail], axis=1), moved, width, 1
        )
        coeff = material(columns + offset, profile, period_seq, inverse)
        field_e, field_hx, field_hz = (extended[0], extended[1], extended[2])
        upper = jnp.concatenate([field_e[:, 1:], zero_col], axis=1)
        field_hx = (field_hx + courant * (upper - field_e)) * inside
        ahead = jnp.concatenate([field_e[1:], zero_row], axis=0)
        field_hz = (field_hz - courant * (ahead - field_e)) * inside
        lower = jnp.concatenate([zero_col, field_hx[:, :-1]], axis=1)
        behind = jnp.concatenate([zero_row, field_hz[:-1]], axis=0)
        field_e = (field_e + courant * coeff * (field_hx - lower - (field_hz - behind))) * inside
        extended = jnp.stack([field_e, field_hx, field_hz])
    return (extended, offset)


def body(electric, magnetic_x, magnetic_z, index_map, period_seq, eps_table, shifts):
    cells_x, cells_z = electric.shape
    total_x = cells_x * lax.axis_size("gx")
    total_z = cells_z * lax.axis_size("gz")
    first_col = lax.axis_index("gx") * cells_x
    first_layer = lax.axis_index("gz") * cells_z
    inverse = 1.0 / eps_table
    fields = jnp.stack([electric, magnetic_x, magnetic_z])
    offset = jnp.int32(0)
    reach = ITERS * (SMAX + 1)
    profile = with_halo(index_map, (("gz", 2),), ITERS)
    lead = passed_along(fields[:, :reach], "gx", -1)
    trail = passed_along(fields[:, cells_x - ITERS :], "gx", 1)
    extended = jnp.concatenate([trail, fields, lead], axis=1)
    extended = with_halo(extended, (("gz", 2),), ITERS)
    extended, offset = advance(
        extended,
        profile,
        period_seq,
        inverse,
        shifts,
        0,
        ITERS,
        first_col - ITERS,
        first_layer - ITERS,
        total_x,
        total_z,
        offset,
    )
    fields = extended[:, ITERS : ITERS + cells_x, ITERS : ITERS + cells_z]
    return (fields[0], fields[1], fields[2])


def solution(mesh):
    placed = (
        P(("grp", "gx"), "gz"),
        P(("grp", "gx"), "gz"),
        P(("grp", "gx"), "gz"),
        P(None, None, "gz"),
        P("grp"),
        P(),
        P("grp"),
    )
    return jax.shard_map(
        body,
        mesh=mesh,
        in_specs=placed,
        out_specs=(P(("grp", "gx"), "gz"), P(("grp", "gx"), "gz"), P(("grp", "gx"), "gz")),
        check_vma=False,
    )
```

profile of v0, /device:TPU:0, one launch (start us, length us, event | category | flops | bytes accessed | tf_op | source)
XLA Modules:
  0.0 103.1 jit_solution(9242696308902369123)
XLA Ops:
  0.7 1.2 %pad_maximum_fusion.3 = f32[3,4,4096]{2,1,0:T(4,128)S(1)} fusion(f32[1,32,4096]{2,1,0:T(8,128)} %bitcast.151, f32[1,32,4096]{2,1,0:T(8,128)} %bitcast.154, f32[1,32,4096]{2,1,0:T(8,128)} %bitcast.157), kind=kLoop, calls=%fused_computation.77 | loop fusion | flops 98304 | bytes 1769472 | tf_op jit(solution)/shard_map/slice | solution.py:104
  1.9 4.9 %collective-permute-start = (f32[3,4,4096]{2,1,0:T(4,128)S(1)}, f32[3,4,4096]{2,1,0:T(4,128)S(1)}, u32[]{:S(2)}, u32[]{:S(2)}) collective-permute-start(f32[3,4,4096]{2,1,0:T(4,128)S(1)} %pad_maximum_fusion.3), channel_id=1, source_target_pairs={{0,2},{2,4},{4,6},{6,8},{8,10},{10,12},{12,14},{1,3},{3,5},{5,7},{... | collective-permute-start | bytes 589832 | tf_op jit(solution)/shard_map/ppermute | solution.py:29
  6.8 1.7 %fusion.51 = (s32[4,64,4]{2,1,0:T(8,128)}, s32[4,64,4]{2,1,0:T(8,128)}) fusion(s32[4,64,4096]{2,1,0:T(8,128)} %param.10), kind=kLoop, calls=%fused_computation.133 | loop fusion | bytes 16384 | tf_op jit(solution)/shard_map/slice | solution.py:21
  8.5 1.3 %collective-permute-start.5 = (s32[4,64,4]{2,1,0:T(8,128)}, s32[4,64,4]{2,1,0:T(8,128)S(1)}, u32[]{:S(2)}, u32[]{:S(2)}) collective-permute-start(s32[4,64,4]{2,1,0:T(8,128)} %get-tuple-element.9), channel_id=1, source_target_pairs={{1,0},{3,2},{5,4},{7,6},{9,8},{11,10},{13,12},{15,14},{17,16},{19,... | collective-permute-start | bytes 12296 | tf_op jit(solution)/shard_map/ppermute | solution.py:21
  9.8 3.0 %collective-permute-start.4 = (s32[4,64,4]{2,1,0:T(8,128)}, s32[4,64,4]{2,1,0:T(8,128)S(1)}, u32[]{:S(2)}, u32[]{:S(2)}) collective-permute-start(s32[4,64,4]{2,1,0:T(8,128)} %get-tuple-element.10), channel_id=1, source_target_pairs={{0,1},{2,3},{4,5},{6,7},{8,9},{10,11},{12,13},{14,15},{16,17},{18,... | collective-permute-start | bytes 12296 | tf_op jit(solution)/shard_map/ppermute | solution.py:18
  12.9 2.3 %pad_maximum_fusion.1 = f32[3,20,4096]{2,1,0:T(8,128)} fusion(f32[1,32,4096]{2,1,0:T(8,128)} %bitcast.152, f32[1,32,4096]{2,1,0:T(8,128)} %bitcast.155, f32[1,32,4096]{2,1,0:T(8,128)} %bitcast.158), kind=kLoop, calls=%fused_computation.44 | loop fusion | flops 491520 | bytes 2555904 | tf_op jit(solution)/shard_map/stack | solution.py:99
  15.2 1.3 %collective-permute-start.1 = (f32[3,20,4096]{2,1,0:T(8,128)}, f32[3,20,4096]{2,1,0:T(8,128)S(1)}, u32[]{:S(2)}, u32[]{:S(2)}) collective-permute-start(f32[3,20,4096]{2,1,0:T(8,128)} %pad_maximum_fusion.1), channel_id=1, source_target_pairs={{2,0},{4,2},{6,4},{8,6},{10,8},{12,10},{14,12},{3,1},{5,3},{7,5},{... | collective-permute-start | bytes 2949128 | tf_op jit(solution)/shard_map/ppermute | solution.py:29
  16.5 0.7 fusion.53
  21.2 0.7 fusion.42
  21.9 22.7 %collective-permute-done.1 = f32[3,20,4096]{2,1,0:T(8,128)S(1)} collective-permute-done((f32[3,20,4096]{2,1,0:T(8,128)}, f32[3,20,4096]{2,1,0:T(8,128)S(1)}, u32[]{:S(2)}, u32[]{:S(2)}) %collective-permute-start.1) | collective-permute-done | bytes 983072 | tf_op jit(solution)/shard_map/ppermute | solution.py:29
  45.0 1.6 %copy-done = f32[3,56,4096]{2,1,0:T(8,128)} copy-done((f32[3,56,4096]{2,1,0:T(8,128)}, f32[3,56,4096]{2,1,0:T(8,128)S(1)}, u32[]{:S(2)}) %copy-start) | copy-done | bytes 2752536
  46.7 1.3 %collective-permute-start.3 = (f32[3,56,4]{2,1,0:T(8,128)S(1)}, f32[3,56,4]{2,1,0:T(8,128)S(1)}, u32[]{:S(2)}, u32[]{:S(2)}) collective-permute-start(f32[3,56,4]{2,1,0:T(8,128)S(1)} %get-tuple-element.17), channel_id=1, source_target_pairs={{1,0},{3,2},{5,4},{7,6},{9,8},{11,10},{13,12},{15,14},{17,16},{19,... | collective-permute-start | bytes 8072 | tf_op jit(solution)/shard_map/ppermute | solution.py:21
  48.0 3.0 %collective-permute-start.2 = (f32[3,56,4]{2,1,0:T(8,128)S(1)}, f32[3,56,4]{2,1,0:T(8,128)S(1)}, u32[]{:S(2)}, u32[]{:S(2)}) collective-permute-start(f32[3,56,4]{2,1,0:T(8,128)S(1)} %get-tuple-element.18), channel_id=1, source_target_pairs={{0,1},{2,3},{4,5},{6,7},{8,9},{10,11},{12,13},{14,15},{16,17},{18,... | collective-permute-start | bytes 8072 | tf_op jit(solution)/shard_map/ppermute | solution.py:18
  58.6 6.4 %concatenate.72 = s32[4,64,4104]{2,1,0:T(8,128)} concatenate(s32[4,64,4]{2,1,0:T(8,128)S(1)} %collective-permute-done.4, s32[4,64,4096]{2,1,0:T(8,128)} %param.10, s32[4,64,4]{2,1,0:T(8,128)S(1)} %collective-permute-done.5), dimensions={2} | concatenate | bytes 8404992 | tf_op jit(solution)/shard_map/concatenate | solution.py:22
  65.0 4.5 %convert_element_type.5 = f32[4,64,4104]{2,1,0:T(8,128)} convert(s32[4,64,4104]{2,1,0:T(8,128)} %concatenate.72) | non-fusion elementwise | flops 1050624 | bytes 8404992 | tf_op jit(solution)/shard_map/convert_element_type | solution.py:41
  69.5 3.5 %concatenate.70 = f32[3,56,4104]{2,1,0:T(8,128)S(1)} concatenate(f32[3,56,4]{2,1,0:T(8,128)S(1)} %collective-permute-done.2, f32[3,56,4096]{2,1,0:T(8,128)} %copy-done, f32[3,56,4]{2,1,0:T(8,128)S(1)} %collective-permute-done.3), dimensions={2} | concatenate | bytes 5515776 | tf_op jit(solution)/shard_map/concatenate | solution.py:22
  74.1 1.2 %slice-done = s8[4194304]{0:T(1024)(128)(4,1)S(1)} async-done(((s8[4325376]{0:T(1024)(128)(4,1)}), s8[4194304]{0:T(1024)(128)(4,1)S(1)}, s32[]{:S(2)}) %slice-start) | async-done | bytes 4194328
  75.4 5.0 %fusion.21 = f32[1,56,4104]{2,1,0:T(8,128)S(1)} fusion(f32[56,4104]{1,0:T(8,128)S(1)} %get-tuple-element.8, f32[56,4104]{1,0:T(8,128)S(1)} %get-tuple-element.7, f32[55,4104]{1,0:T(8,128)S(1)} %bitcast.135, f32[56,4104]{1,0:T(8,128)S(1)} %and_select_fusion.11, f32[56,4103]{1,0:T(8,128)S(1)} %bitcast.137, f32[]{:T(128)} %bitcast.9, f32[]{:T(128)} %bitcast.8, ...), kind=kOutput, calls=%fused_computation.52 | convolution fusion | flops 710400320 | bytes 9706032 | tf_op jit(solution)/shard_map/dot_general | solution.py:42
  81.9 5.1 %fusion.22 = f32[1,56,4104]{2,1,0:T(8,128)S(1)} fusion(f32[56,4104]{1,0:T(8,128)S(1)} %get-tuple-element.16, f32[55,4104]{1,0:T(8,128)S(1)} %bitcast.141, f32[56,4104]{1,0:T(8,128)S(1)} %get-tuple-element.15, f32[56,4103]{1,0:T(8,128)S(1)} %bitcast.139, f32[]{:T(128)} %bitcast.9, f32[]{:T(128)} %bitcast.8, f32[]{:T(128)} %bitcast.7, f32[]{:T(128)} %bitcast.6, ...), kind=kOutput, calls=%fused_computation.53 | convolution fusion | flops 710400320 | bytes 9706032 | tf_op jit(solution)/shard_map/dot_general | solution.py:42
  88.4 5.1 %fusion.23 = f32[1,56,4104]{2,1,0:T(8,128)S(1)} fusion(f32[56,4104]{1,0:T(8,128)S(1)} %get-tuple-element.14, f32[55,4104]{1,0:T(8,128)S(1)} %bitcast.145, f32[56,4104]{1,0:T(8,128)S(1)} %get-tuple-element.13, f32[56,4103]{1,0:T(8,128)S(1)} %bitcast.143, f32[]{:T(128)} %bitcast.9, f32[]{:T(128)} %bitcast.8, f32[]{:T(128)} %bitcast.7, f32[]{:T(128)} %bitcast.6, ...), kind=kOutput, calls=%fused_computation.54 | convolution fusion | flops 710400320 | bytes 9706032 | tf_op jit(solution)/shard_map/dot_general | solution.py:42
  95.1 5.0 %fusion.24 = f32[1,56,4104]{2,1,0:T(8,128)S(1)} fusion(f32[56,4104]{1,0:T(8,128)S(1)} %get-tuple-element.12, f32[55,4104]{1,0:T(8,128)S(1)} %bitcast.149, f32[56,4104]{1,0:T(8,128)S(1)} %get-tuple-element.11, f32[56,4103]{1,0:T(8,128)S(1)} %bitcast.147, f32[]{:T(128)} %bitcast.9, f32[]{:T(128)} %bitcast.8, f32[]{:T(128)} %bitcast.7, f32[]{:T(128)} %bitcast.6, ...), kind=kOutput, calls=%fused_computation.55 | convolution fusion | flops 710400320 | bytes 9706032 | tf_op jit(solution)/shard_map/dot_general | solution.py:42
  100.1 1.0 slice_bitcast_fusion.14
  101.1 1.0 slice_bitcast_fusion.12
  102.1 1.0 slice_bitcast_fusion.13
  (53 shorter events, 7.5 us)
Async XLA Ops:
  0.6 43.9 %copy-start.1 = (f32[32,4096]{1,0:T(8,128)S(1)}, f32[32,4096]{1,0:T(8,128)}, u32[]{:S(2)}) copy-start(f32[32,4096]{1,0:T(8,128)} %param.9) | copy-start | bytes 1572868
  0.6 43.9 %copy-start.2 = (f32[32,4096]{1,0:T(8,128)S(1)}, f32[32,4096]{1,0:T(8,128)}, u32[]{:S(2)}) copy-start(f32[32,4096]{1,0:T(8,128)} %param.8) | copy-start | bytes 1572868
  0.7 43.9 %copy-start.3 = (f32[32,4096]{1,0:T(8,128)S(1)}, f32[32,4096]{1,0:T(8,128)}, u32[]{:S(2)}) copy-start(f32[32,4096]{1,0:T(8,128)} %param.7) | copy-start | bytes 1572868
  0.7 15.8 %copy-start.6 = (f32[4]{0:T(128)S(1)}, f32[4]{0:T(128)}, u32[]{:S(2)}) copy-start(f32[4]{0:T(128)} %param.12) | copy-start | bytes 52
  0.7 16.5 %copy-start.4 = (s32[4]{0:T(128)S(1)}, s32[4]{0:T(128)}, u32[]{:S(2)}) copy-start(s32[4]{0:T(128)} %param.13) | copy-start | bytes 52
  0.7 20.4 %copy-start.5 = (s32[5]{0:T(128)S(1)}, s32[5]{0:T(128)}, u32[]{:S(2)}) copy-start(s32[5]{0:T(128)} %param.11) | copy-start | bytes 64
  1.9 20.0 %collective-permute-start = (f32[3,4,4096]{2,1,0:T(4,128)S(1)}, f32[3,4,4096]{2,1,0:T(4,128)S(1)}, u32[]{:S(2)}, u32[]{:S(2)}) collective-permute-start(f32[3,4,4096]{2,1,0:T(4,128)S(1)} %pad_maximum_fusion.3), channel_id=1, source_target_pairs={{0,2},{2,4},{4,6},{6,8},{8,10},{10,12},{12,14},{1,3},{3,5},{5,7},{... | collective-permute-start | bytes 589832 | tf_op jit(solution)/shard_map/ppermute | solution.py:29
  8.5 50.1 %collective-permute-start.5 = (s32[4,64,4]{2,1,0:T(8,128)}, s32[4,64,4]{2,1,0:T(8,128)S(1)}, u32[]{:S(2)}, u32[]{:S(2)}) collective-permute-start(s32[4,64,4]{2,1,0:T(8,128)} %get-tuple-element.9), channel_id=1, source_target_pairs={{1,0},{3,2},{5,4},{7,6},{9,8},{11,10},{13,12},{15,14},{17,16},{19,... | collective-permute-start | bytes 12296 | tf_op jit(solution)/shard_map/ppermute | solution.py:21
  9.8 48.8 %collective-permute-start.4 = (s32[4,64,4]{2,1,0:T(8,128)}, s32[4,64,4]{2,1,0:T(8,128)S(1)}, u32[]{:S(2)}, u32[]{:S(2)}) collective-permute-start(s32[4,64,4]{2,1,0:T(8,128)} %get-tuple-element.10), channel_id=1, source_target_pairs={{0,1},{2,3},{4,5},{6,7},{8,9},{10,11},{12,13},{14,15},{16,17},{18,... | collective-permute-start | bytes 12296 | tf_op jit(solution)/shard_map/ppermute | solution.py:18
  15.2 29.3 %collective-permute-start.1 = (f32[3,20,4096]{2,1,0:T(8,128)}, f32[3,20,4096]{2,1,0:T(8,128)S(1)}, u32[]{:S(2)}, u32[]{:S(2)}) collective-permute-start(f32[3,20,4096]{2,1,0:T(8,128)} %pad_maximum_fusion.1), channel_id=1, source_target_pairs={{2,0},{4,2},{6,4},{8,6},{10,8},{12,10},{14,12},{3,1},{5,3},{7,5},{... | collective-permute-start | bytes 2949128 | tf_op jit(solution)/shard_map/ppermute | solution.py:29
  45.0 1.6 %copy-start = (f32[3,56,4096]{2,1,0:T(8,128)}, f32[3,56,4096]{2,1,0:T(8,128)S(1)}, u32[]{:S(2)}) copy-start(f32[3,56,4096]{2,1,0:T(8,128)S(1)} %pad_maximum_fusion) | copy-start | bytes 8257540
  46.7 22.9 %collective-permute-start.3 = (f32[3,56,4]{2,1,0:T(8,128)S(1)}, f32[3,56,4]{2,1,0:T(8,128)S(1)}, u32[]{:S(2)}, u32[]{:S(2)}) collective-permute-start(f32[3,56,4]{2,1,0:T(8,128)S(1)} %get-tuple-element.17), channel_id=1, source_target_pairs={{1,0},{3,2},{5,4},{7,6},{9,8},{11,10},{13,12},{15,14},{17,16},{19,... | collective-permute-start | bytes 8072 | tf_op jit(solution)/shard_map/ppermute | solution.py:21
  48.0 21.6 %collective-permute-start.2 = (f32[3,56,4]{2,1,0:T(8,128)S(1)}, f32[3,56,4]{2,1,0:T(8,128)S(1)}, u32[]{:S(2)}, u32[]{:S(2)}) collective-permute-start(f32[3,56,4]{2,1,0:T(8,128)S(1)} %get-tuple-element.18), channel_id=1, source_target_pairs={{0,1},{2,3},{4,5},{6,7},{8,9},{10,11},{12,13},{14,15},{16,17},{18,... | collective-permute-start | bytes 8072 | tf_op jit(solution)/shard_map/ppermute | solution.py:18
  73.2 2.2 %slice-start = ((s8[4325376]{0:T(1024)(128)(4,1)}), s8[4194304]{0:T(1024)(128)(4,1)S(1)}, s32[]{:S(2)}) async-start(s8[4325376]{0:T(1024)(128)(4,1)} %bitcast.129), calls=%async_computation | async-start | bytes 8388608
  73.5 1.9 %slice-start.1 = ((s8[4325376]{0:T(1024)(128)(4,1)}), s8[131072]{0:T(1024)(128)(4,1)S(1)}, s32[]{:S(2)}) async-start(s8[4325376]{0:T(1024)(128)(4,1)} %bitcast.129), calls=%async_computation.1 | async-start | bytes 262144
where the time goes:
time: 104 us; the launch traced here: 103 us
  waiting for transfers between devices  22.7 us (22%)
  local copies, waits for them, and re-layouts  20.6 us (20%)
  matrix products  20.2 us (19%)
  starting transfers between devices  14.8 us (14%)
  other arithmetic  13.7 us (13%)
  between operations  11.1 us (11%)
    ppermute x2, waiting for transfers between devices, passed_along(): return lax.ppermute(block, axis, route)  22.7 us
    dot_general x4, matrix products, material(): levels = jnp.dot(onehot, table, precision=lax.Precision.HIGHEST)  20.2 us
    concatenate x2, local copies, waits for them, and re-layouts, with_halo(): block = jnp.concatenate([low, block, high], axis=dim)  9.92 us
    ppermute x2, starting transfers between devices, passed_along(): return lax.ppermute(block, axis, route)  6.19 us
    ppermute x2, starting transfers between devices, with_halo(): lax.ppermute(lax.slice_in_dim(block, block.shape[dim] - width, None, axis...  6.08 us
    convert_element_type x1, other arithmetic, material(): table = profile.reshape(rows_all, profile.shape[2]).astype(jnp.float32)  4.51 us
    squeeze x3, local copies, waits for them, and re-layouts, body(): return (fields[0], fields[1], fields[2])  2.99 us
    unnamed x18, local copies, waits for them, and re-layouts  2.88 us
  transfers between devices with their start and end apart: 6, of which 1 were waited for; matrix products, arithmetic and copies ran while one was open for 18% of the time, Pallas kernels for 0%

commit v1 on v0

v1 whole, which is shorter than its diff:
```python
import functools

import jax
import jax.numpy as jnp
from jax import lax
from jax.experimental import pallas as pl
from jax.experimental.pallas import tpu as pltpu
from jax.sharding import PartitionSpec as P

ITERS = 4
SMAX = 4
LANES = 128
TILE = 8
OUTER = 16

courant = 0.6

VMEM = pltpu.VMEM
ANY = pl.ANY


def up(value, unit):
    return -(-value // unit) * unit


def spec(space):
    return pl.BlockSpec(memory_space=space)


def sides(gz):
    return gz == 0


def pack_kernel(plan, part, e, hx, hz, out, buf, sem):
    low = lax.axis_index("gz") == 0
    count = plan.count[part]
    start = jnp.where(low, plan.start_low[part], plan.start_high[part]) * LANES
    start = pl.multiple_of(start, LANES)
    rows = buf.shape[1]
    copies = [
        pltpu.make_async_copy(
            field.at[pl.ds(0, rows), pl.ds(start, count * LANES)], buf.at[i], sem.at[i]
        )
        for i, field in enumerate((e, hx, hz))
    ]
    for copy in copies:
        copy.start()
    for copy in copies:
        copy.wait()
    for strip in range(count):
        for i in range(3):
            for q in range(rows // TILE):
                at = strip * plan.sent + plan.place[i] + q * TILE
                out[pl.ds(at, TILE), :] = buf[i, pl.ds(q * TILE, TILE), pl.ds(strip * LANES, LANES)]


def material_of(levels, inverse):
    result = jnp.zeros(levels.shape, jnp.float32)
    for level, value in enumerate(inverse):
        result = jnp.where(levels == level, value, result)
    return result


def inverse_table(eps):
    return [courant * (1.0 / jnp.full((TILE, LANES), eps[i], jnp.float32)) for i in range(eps.shape[0])]


def map_rows(plan, period_seq, index_map, group, first, width):
    span = index_map.shape[1]
    cell = lax.axis_index("gx") * plan.rows + group * TILE
    period = jnp.minimum(cell // span, period_seq.shape[0] - 1)
    phase = pl.multiple_of(cell % span, TILE)
    return index_map.at[period_seq[period], pl.ds(phase, TILE), pl.ds(first, width)]


def edge_kernel(plan, period_seq, eps, e, hx, hz, index_map, out, levels, sem):
    low = lax.axis_index("gz") == 0
    first = pl.multiple_of(jnp.where(low, plan.strips - 1, 0) * LANES, LANES)
    rows = plan.rows
    copies = [
        pltpu.make_async_copy(
            field.at[:, pl.ds(first, LANES)], out.at[pl.ds(i * rows, rows), :], sem.at[i]
        )
        for i, field in enumerate((e, hx, hz))
    ]
    for group in range(plan.reach // TILE):
        copies.append(
            pltpu.make_async_copy(
                map_rows(plan, period_seq, index_map, group, first, LANES),
                levels.at[pl.ds(group * TILE, TILE), :],
                sem.at[3 + group],
            )
        )
    for copy in copies:
        copy.start()
    for copy in copies:
        copy.wait()
    inverse = inverse_table(eps)
    for group in range(plan.reach // TILE):
        at = pl.ds(group * TILE, TILE)
        out[pl.ds(3 * rows + group * TILE, TILE), :] = material_of(levels[at, :], inverse)


def prepare_kernel(plan, period_seq, eps, e, hx, hz, index_map, e_out, hx_out, hz_out, coeff, levels, sem):
    width = plan.strips * LANES
    fields = [
        pltpu.make_async_copy(src, dst, sem.at[i])
        for i, (src, dst) in enumerate(((e, e_out), (hx, hx_out), (hz, hz_out)))
    ]
    groups = plan.reach // TILE
    maps = [
        pltpu.make_async_copy(
            map_rows(plan, period_seq, index_map, group, 0, width),
            levels.at[pl.ds(group * TILE, TILE), :],
            sem.at[3 + group],
        )
        for group in range(groups)
    ]
    for copy in maps + fields:
        copy.start()
    inverse = inverse_table(eps)
    for group in range(groups):
        maps[group].wait()
        at = pl.ds(group * TILE, TILE)

        def strip_of(strip, _, at=at):
            lanes = pl.ds(pl.multiple_of(strip * LANES, LANES), LANES)
            coeff[at, lanes] = material_of(levels[at, lanes], inverse)
            return 0

        lax.fori_loop(0, plan.strips, strip_of, 0, unroll=8)
    for copy in fields:
        copy.wait()


def update_kernel(plan, part, shifts, *refs):
    fields, coeff, halo, halo_lead, leads = refs[0:3], refs[3], refs[4], refs[5], refs[6 : 7 + part]
    refs = refs[7 + part :]
    if part:
        refs = refs[3:]
    outs, work, work_coeff, stage, sem = refs[0:3], refs[3:6], refs[6], refs[7], refs[8]
    low = lax.axis_index("gz") == 0
    rows, reach, strips = plan.rows, plan.reach, plan.strips
    lead_rows = reach - rows
    local = plan.local[part]

    def own(strip, to):
        lanes = pl.ds(pl.multiple_of(strip * LANES, LANES), LANES)
        for i in range(3):
            work[i][to, pl.ds(0, rows), :] = fields[i][:, lanes]
        work_coeff[to] = coeff[:, lanes]

    def lead(source, at, to):
        for i in range(3):
            for q in range(lead_rows // TILE):
                work[i][to, pl.ds(rows + q * TILE, TILE), :] = source[pl.ds(at + plan.place[i] + q * TILE, TILE), :]

    for i in range(3):
        work[i][local] = jnp.zeros((reach, LANES), jnp.float32)
    inner, outer = plan.count
    if part == 0:
        shift = jnp.where(low, 0, 1)
        first = jnp.where(low, outer, 0)

        def gather(k, _):
            own(first + k, shift + k)
            lead(leads[0], k * plan.sent, shift + k)
            return 0

        lax.fori_loop(0, inner, gather, 0)
        side = jnp.where(low, inner, 0)
        for i in range(3):
            work[i][side, pl.ds(0, rows), :] = halo[pl.ds(i * rows, rows), :]
        work_coeff[side] = halo[pl.ds(3 * rows, reach), :]
        lead(halo_lead, 0, side)
        done, kept = 1, inner - 1
        column = jnp.where(low, outer + 1, 0)
    else:
        shift = jnp.where(low, 0, 2)
        first = jnp.where(low, 0, inner)

        def gather(k, _):
            own(first + k, shift + k)
            lead(leads[1], k * plan.sent, shift + k)
            return 0

        lax.fori_loop(0, outer, gather, 0)
        for k in range(2):
            strip = jnp.where(low, outer + k, inner - 2 + k)
            to = jnp.where(low, outer + k, k)
            own(strip, to)
            lead(leads[0], jnp.where(low, k, inner - 2 + k) * plan.sent, to)
        done, kept = jnp.where(low, 0, 1), outer + 1
        column = jnp.where(low, 0, inner - 1)

    row = lax.broadcasted_iota(jnp.int32, (reach, LANES), 0)
    lane = lax.broadcasted_iota(jnp.int32, (reach, LANES), 1)
    start = lax.axis_index("gx") * rows
    total = lax.axis_size("gx") * rows
    offset = jnp.int32(0)
    for step in range(ITERS):
        offset = offset + shifts[step]
        above = row >= offset - start
        below = row < offset + total - start

        def strip_step(strip, carry):
            turned, hx_before = carry
            field_e = work[0][strip]
            turned_next = pltpu.roll(work[0][strip + 1], LANES - 1, 1)
            upper = jnp.where(lane == LANES - 1, turned_next, turned)
            field_hx = work[1][strip] + courant * (upper - field_e)
            ahead = pltpu.roll(field_e, reach - 1, 0)
            field_hz = work[2][strip] - courant * (ahead - field_e)
            field_hz = jnp.where(above, field_hz, 0.0)
            hx_turned = pltpu.roll(field_hx, 1, 1)
            lower = jnp.where(lane == 0, hx_before, hx_turned)
            behind = pltpu.roll(field_hz, 1, 0)
            moved = field_e + work_coeff[strip] * ((field_hx - lower) - (field_hz - behind))
            work[0][strip] = jnp.where(below, moved, 0.0)
            work[1][strip] = field_hx
            work[2][strip] = field_hz
            return turned_next, hx_turned

        none = jnp.zeros((reach, LANES), jnp.float32)
        lax.fori_loop(0, local, strip_step, (pltpu.roll(work[0][0], LANES - 1, 1), none))

    def finish(k, _):
        lanes = pl.ds(pl.multiple_of(k * LANES, LANES), LANES)
        for i in range(3):
            for q in range(rows // TILE):
                stage[i, pl.ds(q * TILE, TILE), lanes] = work[i][done + k, pl.ds(offset + q * TILE, TILE), :]
        return 0

    lax.fori_loop(0, kept, finish, 0)
    column = pl.multiple_of(column * LANES, LANES)
    copies = [
        pltpu.make_async_copy(stage.at[i], outs[i].at[:, pl.ds(column, kept * LANES)], sem.at[i])
        for i in range(3)
    ]
    for copy in copies:
        copy.start()
    for copy in copies:
        copy.wait()


class Plan:
    def __init__(self, rows, cols, moved):
        self.rows = rows
        self.strips = cols // LANES
        self.reach = up(rows + ITERS * SMAX + ITERS, TILE)
        outer = OUTER
        inner = self.strips - outer
        self.count = (inner, outer)
        self.start_low = (outer, 0)
        self.start_high = (0, inner)
        self.local = (inner + 1, outer + 2)
        lead_e, lead_h = moved + ITERS, moved + ITERS - 1
        self.place = (0, lead_e, lead_e + lead_h)
        self.sent = lead_e + 2 * lead_h
        self.head = up(lead_e, TILE)

        self.window = up(self.place[2] + self.reach - rows, TILE)

    def buffer(self, part):
        return up((self.count[part] - 1) * self.sent + self.window, TILE)


def call(kernel, name, outs, ins, out_spaces, scratch, aliases=None, flops=1):
    return pl.pallas_call(
        kernel,
        name=name,
        out_shape=outs,
        in_specs=[spec(space) for space in ins],
        out_specs=[spec(space) for space in out_spaces],
        scratch_shapes=scratch,
        input_output_aliases=aliases or {},
        cost_estimate=pl.CostEstimate(flops=flops, bytes_accessed=flops, transcendentals=0),
        compiler_params=pltpu.CompilerParams(vmem_limit_bytes=16 << 20),
    )


def f32(*shape):
    return jax.ShapeDtypeStruct(shape, jnp.float32)


def advance(moved, electric, magnetic_x, magnetic_z, index_map, period_seq, eps_table, shifts):
    rows, cols = electric.shape
    plan = Plan(rows, cols, moved)
    strips, reach = plan.strips, plan.reach
    fields = (electric, magnetic_x, magnetic_z)
    count_x = lax.axis_size("gx")
    back = [(i + 1, i) for i in range(count_x - 1)]
    swap = [(0, 1), (1, 0)]
    leads = []
    for part in range(2):
        packed = call(
            functools.partial(pack_kernel, plan, part),
            f"pack{part}",
            [f32(plan.buffer(part), LANES)],
            [ANY] * 3,
            [VMEM],
            [VMEM((3, plan.head, plan.count[part] * LANES), jnp.float32), pltpu.SemaphoreType.DMA((3,))],
        )(*fields)[0]
        leads.append(lax.ppermute(packed, "gx", back))
    groups = reach // TILE
    edge = call(
        functools.partial(edge_kernel, plan),
        "edge",
        [f32(3 * rows + reach, LANES)],
        [pltpu.SMEM] * 2 + [ANY] * 4,
        [VMEM],
        [VMEM((reach, LANES), jnp.int32), pltpu.SemaphoreType.DMA((3 + groups,))],
    )(period_seq, eps_table, *fields, index_map)[0]
    halo = lax.ppermute(edge, "gz", swap)
    *held, coeff = call(
        functools.partial(prepare_kernel, plan),
        "prepare",
        [f32(rows, cols)] * 3 + [f32(reach, cols)],
        [pltpu.SMEM] * 2 + [ANY] * 4,
        [VMEM] * 4,
        [VMEM((reach, cols), jnp.int32), pltpu.SemaphoreType.DMA((3 + groups,))],
    )(period_seq, eps_table, *fields, index_map)
    at = jnp.where(lax.axis_index("gz") == 0, plan.count[0] - 1, 0) * plan.sent
    halo_lead = lax.ppermute(
        lax.dynamic_slice_in_dim(leads[0], at, plan.window, 0), "gz", swap
    )
    outs = ()
    for part in range(2):
        kept = (plan.count[0] - 1, plan.count[1] + 1)[part]
        work = [VMEM((plan.local[part] + 1, reach, LANES), jnp.float32)] * 4
        outs = call(
            functools.partial(update_kernel, plan, part),
            f"update{part}",
            [f32(rows, cols)] * 3,
            [pltpu.SMEM] + [VMEM] * (7 + part) + [ANY] * len(outs),
            [ANY] * 3,
            work + [VMEM((3, rows, kept * LANES), jnp.float32), pltpu.SemaphoreType.DMA((3,))],
            {8 + part + i: i for i in range(len(outs))},
        )(shifts, *held, coeff, halo, halo_lead, *leads[: 1 + part], *outs)
    return tuple(outs)


def body(electric, magnetic_x, magnetic_z, index_map, period_seq, eps_table, shifts):
    return advance(ITERS * SMAX, electric, magnetic_x, magnetic_z, index_map, period_seq, eps_table, shifts)


def solution(mesh):
    assert mesh.shape["gz"] == 2
    placed = (
        P(("grp", "gx"), "gz"),
        P(("grp", "gx"), "gz"),
        P(("grp", "gx"), "gz"),
        P(None, None, "gz"),
        P("grp"),
        P(),
        P("grp"),
    )
    return jax.shard_map(
        body,
        mesh=mesh,
        in_specs=placed,
        out_specs=(P(("grp", "gx"), "gz"), P(("grp", "gx"), "gz"), P(("grp", "gx"), "gz")),
        check_vma=False,
    )
```

time: 104 us -> 53.3 us (0.51)
  Pallas kernels: 0 us -> 31 us
  matrix products: 20.2 us -> 0 us
  waiting for transfers between devices: 22.7 us -> 8.25 us
  other arithmetic: 13.7 us -> 0 us
  local copies, waits for them, and re-layouts: 20.6 us -> 8.84 us
  starting transfers between devices: 14.8 us -> 3.34 us
  between operations: 11.1 us -> 0.84 us
    pallas_call x0 -> x6, Pallas kernels: none -> 31 us  [the longest x2 26.5 us: advance(): call(functools.partial(update_kernel, plan, part), f'update{part}', [f32(...]
    dot_general x4 -> x0, matrix products: 20.2 us -> none  [material(): levels = jnp.dot(onehot, table, precision=lax.Precision.HIGHEST)]
    ppermute x6 -> x4, waiting for transfers between devices: 22.7 us -> 8.25 us  [the longest x2 8.24 us: advance(): leads.append(lax.ppermute(packed, 'gx', back))]
    ppermute x6 -> x4, starting transfers between devices: 14.8 us -> 3.34 us  [the longest x2 2.72 us: advance(): leads.append(lax.ppermute(packed, 'gx', back))]
    concatenate x2 -> x0, local copies, waits for them, and re-layouts: 9.92 us -> none  [with_halo(): block = jnp.concatenate([low, block, high], axis=dim)]
    unnamed x18 -> x26, local copies, waits for them, and re-layouts: 2.88 us -> 8.83 us
    slice x12 -> x0, local copies, waits for them, and re-layouts: 4.66 us -> none  [the longest x2 1.81 us: with_halo(): lax.slice_in_dim(block, 0, width, axis=dim)]
    convert_element_type x1 -> x0, other arithmetic: 4.51 us -> none  [material(): table = profile.reshape(rows_all, profile.shape[2]).astype(jnp.float32)]
  transfers between devices with their start and end apart: 6 -> 4, of which waited for: 1 -> 1; matrix products, arithmetic and copies ran while one was open for 18% -> 0% of each run, Pallas kernels for 0% -> 33%
where the time goes in v1:
time: 53.3 us; the launch traced here: 52.3 us
  Pallas kernels  31 us (58%)
  local copies, waits for them, and re-layouts  8.84 us (17%)
  waiting for transfers between devices  8.25 us (15%)
  starting transfers between devices  3.34 us (6%)
  between operations  0.84 us (2%)
    pallas_call x2, Pallas kernels, advance(): call(functools.partial(update_kernel, plan, part), f'update{part}', [f32(...  26.5 us
    unnamed x26, local copies, waits for them, and re-layouts  8.83 us
    ppermute x2, waiting for transfers between devices, advance(): leads.append(lax.ppermute(packed, 'gx', back))  8.24 us
    ppermute x2, starting transfers between devices, advance(): leads.append(lax.ppermute(packed, 'gx', back))  2.72 us
    pallas_call x1, Pallas kernels, advance(): call(functools.partial(prepare_kernel, plan), 'prepare', [f32(rows, cols)...  2.45 us
    pallas_call x1, Pallas kernels, advance(): call(functools.partial(edge_kernel, plan), 'edge', [f32(3 * rows + reach,...  1.43 us
  transfers between devices with their start and end apart: 4, of which 1 were waited for; matrix products, arithmetic and copies ran while one was open for 0% of the time, Pallas kernels for 33%

profile of v1, /device:TPU:0, one launch (start us, length us, event | category | flops | bytes accessed | tf_op | source)
XLA Modules:
  0.0 52.3 jit_solution(831299824145776337)
XLA Ops:
  0.6 1.0 %copy-done.2 = f32[32,4096]{1,0:T(8,128)S(1)} copy-done((f32[32,4096]{1,0:T(8,128)S(1)}, f32[32,4096]{1,0:T(8,128)}, u32[]{:S(2)}) %copy-start.2) | copy-done | bytes 524312
  1.7 1.0 %copy-done.4 = f32[32,4096]{1,0:T(8,128)S(1)} copy-done((f32[32,4096]{1,0:T(8,128)S(1)}, f32[32,4096]{1,0:T(8,128)}, u32[]{:S(2)}) %copy-start.4) | copy-done | bytes 524312
  2.7 1.0 %copy-done.6 = f32[32,4096]{1,0:T(8,128)S(1)} copy-done((f32[32,4096]{1,0:T(8,128)S(1)}, f32[32,4096]{1,0:T(8,128)}, u32[]{:S(2)}) %copy-start.6) | copy-done | bytes 524312
  3.8 0.3 pack0.1
  4.1 0.0 copy-start.5
  4.1 0.0 copy-start.7
  4.1 0.0 copy-start.9
  4.1 0.0 copy-start.11
  4.1 1.4 %collective-permute-start.1 = (f32[936,128]{1,0:T(8,128)S(1)}, f32[936,128]{1,0:T(8,128)S(1)}, u32[]{:S(2)}, u32[]{:S(2)}) collective-permute-start(f32[936,128]{1,0:T(8,128)S(1)} %pack0.1), channel_id=1, source_target_pairs={{2,0},{4,2},{6,4},{8,6},{10,8},{12,10},{14,12},{3,1},{5,3},{7,5},{... | collective-permute-start | bytes 1437704 | tf_op jit(solution)/shard_map/ppermute | solution.py:304
  5.6 0.3 pack1.1
  5.9 1.3 %collective-permute-start.3 = (f32[936,128]{1,0:T(8,128)S(1)}, f32[936,128]{1,0:T(8,128)S(1)}, u32[]{:S(2)}, u32[]{:S(2)}) collective-permute-start(f32[936,128]{1,0:T(8,128)S(1)} %pack1.1), channel_id=1, source_target_pairs={{2,0},{4,2},{6,4},{8,6},{10,8},{12,10},{14,12},{3,1},{5,3},{7,5},{... | collective-permute-start | bytes 1437704 | tf_op jit(solution)/shard_map/ppermute | solution.py:304
  7.2 0.0 copy-start
  7.2 2.2 %copy-done = s32[4,64,4096]{2,1,0:T(8,128)S(1)} copy-done((s32[4,64,4096]{2,1,0:T(8,128)S(1)}, s32[4,64,4096]{2,1,0:T(8,128)}, u32[]{:S(2)}) %copy-start) | copy-done | bytes 4194328
  9.4 0.7 %copy-done.8 = s32[5]{0:T(128)S(1)} copy-done((s32[5]{0:T(128)S(1)}, s32[5]{0:T(128)}, u32[]{:S(2)}) %copy-start.8) | copy-done | bytes 44
  10.1 0.7 %copy-done.10 = f32[4]{0:T(128)S(1)} copy-done((f32[4]{0:T(128)S(1)}, f32[4]{0:T(128)}, u32[]{:S(2)}) %copy-start.10) | copy-done | bytes 40
  10.7 1.4 %edge.1 = f32[152,128]{1,0:T(8,128)} custom-call(s32[5]{0:T(128)S(1)} %copy-done.8, f32[4]{0:T(128)S(1)} %copy-done.10, f32[32,4096]{1,0:T(8,128)S(1)} %copy-done.3, f32[32,4096]{1,0:T(8,128)S(1)} %copy-done.4, f32[32,4096]{1,0:T(8,128)S(1)} %copy-done.6, s32[4,64,4096]{2,1,0:T(8,128)S(1)} %copy-done), custom_call_target="tpu_custom_call" | custom-call | flops 1 | bytes 1 | tf_op jit(solution)/shard_map/edge/pallas_call | solution.py:306
  12.2 0.0 copy-start.12
  12.2 0.6 %collective-permute-start = (f32[152,128]{1,0:T(8,128)}, f32[152,128]{1,0:T(8,128)}, u32[]{:S(2)}, u32[]{:S(2)}) collective-permute-start(f32[152,128]{1,0:T(8,128)} %edge.1), channel_id=1, source_target_pairs={{0,1},{1,0},{2,3},{3,2},{4,5},{5,4},{6,7},{7,6},{8,9},{9,8},{10,11... | collective-permute-start | bytes 233480 | tf_op jit(solution)/shard_map/ppermute | solution.py:314
  12.7 8.2 %collective-permute-done.1.refs_6_ = f32[936,128]{1,0:T(8,128)S(1)} collective-permute-done((f32[936,128]{1,0:T(8,128)S(1)}, f32[936,128]{1,0:T(8,128)S(1)}, u32[]{:S(2)}, u32[]{:S(2)}) %collective-permute-start.1) | collective-permute-done | bytes 479264 | tf_op jit(solution)/shard_map/ppermute | solution.py:304
  21.0 0.1 collective-permute-start.2
  21.1 2.2 %copy-done.1 = s32[4,64,4096]{2,1,0:T(8,128)S(1)} copy-done((s32[4,64,4096]{2,1,0:T(8,128)S(1)}, s32[4,64,4096]{2,1,0:T(8,128)}, u32[]{:S(2)}) %copy-start.1) | copy-done | bytes 4194328
  23.3 2.5 %prepare.1 = (f32[32,4096]{1,0:T(8,128)S(1)}, f32[32,4096]{1,0:T(8,128)S(1)}, f32[32,4096]{1,0:T(8,128)S(1)}, f32[56,4096]{1,0:T(8,128)S(1)}) custom-call(s32[5]{0:T(128)S(1)} %copy-done.9, f32[4]{0:T(128)S(1)} %copy-done.11, f32[32,4096]{1,0:T(8,128)S(1)} %copy-done.3, f32[32,4096]{1,0:T(8,128)S(1)} %copy-done.5, f32[32,4096]{1,0:T(8,128)S(1)} %copy-done.7, ...), custom_call_target="tpu_custom_call" | custom-call | flops 1 | bytes 1 | tf_op jit(solution)/shard_map/prepare/pallas_call | solution.py:315
  25.8 12.8 %update0.1 = (f32[32,4096]{1,0:T(8,128)}, f32[32,4096]{1,0:T(8,128)}, f32[32,4096]{1,0:T(8,128)}) custom-call(s32[4]{0:T(128)S(1)} %copy-done.12, f32[32,4096]{1,0:T(8,128)S(1)} %get-tuple-element.10.refs_0_, f32[32,4096]{1,0:T(8,128)S(1)} %get-tuple-element.11.refs_1_, f32[32,4096]{1,0:T(8,128)S(1)} %get-tuple-element.12.refs_2_, ...), custom_call_target="tpu_custom_call" | custom-call | flops 1 | bytes 1 | tf_op jit(solution)/shard_map/update0/pallas_call | solution.py:331
  38.6 13.6 %update1.1 = (f32[32,4096]{1,0:T(8,128)}, f32[32,4096]{1,0:T(8,128)}, f32[32,4096]{1,0:T(8,128)}) custom-call(s32[4]{0:T(128)S(1)} %copy-done.12, f32[32,4096]{1,0:T(8,128)S(1)} %get-tuple-element.10.refs_0_, f32[32,4096]{1,0:T(8,128)S(1)} %get-tuple-element.11.refs_1_, ...), custom_call_target="tpu_custom_call", output_to_operand_aliasing={{0}: (9, {}), {1}: (10, {}), {2}: (11, {})} | custom-call | flops 1 | bytes 1 | tf_op jit(solution)/shard_map/update1/pallas_call | solution.py:331
  (17 shorter events, 0.0 us)
Async XLA Ops:
  0.6 1.0 %copy-start.2 = (f32[32,4096]{1,0:T(8,128)S(1)}, f32[32,4096]{1,0:T(8,128)}, u32[]{:S(2)}) copy-start(f32[32,4096]{1,0:T(8,128)} %e.7) | copy-start | bytes 1572868
  1.7 1.0 %copy-start.4 = (f32[32,4096]{1,0:T(8,128)S(1)}, f32[32,4096]{1,0:T(8,128)}, u32[]{:S(2)}) copy-start(f32[32,4096]{1,0:T(8,128)} %hx.7) | copy-start | bytes 1572868
  2.7 1.0 %copy-start.6 = (f32[32,4096]{1,0:T(8,128)S(1)}, f32[32,4096]{1,0:T(8,128)}, u32[]{:S(2)}) copy-start(f32[32,4096]{1,0:T(8,128)} %hz.7) | copy-start | bytes 1572868
  3.8 3.4 %copy-start.3 = (f32[32,4096]{1,0:T(8,128)S(1)}, f32[32,4096]{1,0:T(8,128)}, u32[]{:S(2)}) copy-start(f32[32,4096]{1,0:T(8,128)} %e.7) | copy-start | bytes 1572868
  4.1 17.0 %copy-start.5 = (f32[32,4096]{1,0:T(8,128)S(1)}, f32[32,4096]{1,0:T(8,128)}, u32[]{:S(2)}) copy-start(f32[32,4096]{1,0:T(8,128)} %hx.7) | copy-start | bytes 1572868
  4.1 17.0 %copy-start.7 = (f32[32,4096]{1,0:T(8,128)S(1)}, f32[32,4096]{1,0:T(8,128)}, u32[]{:S(2)}) copy-start(f32[32,4096]{1,0:T(8,128)} %hz.7) | copy-start | bytes 1572868
  4.1 17.0 %copy-start.9 = (s32[5]{0:T(128)S(1)}, s32[5]{0:T(128)}, u32[]{:S(2)}) copy-start(s32[5]{0:T(128)} %period_seq.3) | copy-start | bytes 64
  4.1 17.0 %copy-start.11 = (f32[4]{0:T(128)S(1)}, f32[4]{0:T(128)}, u32[]{:S(2)}) copy-start(f32[4]{0:T(128)} %eps.3) | copy-start | bytes 52
  4.1 16.8 %collective-permute-start.1 = (f32[936,128]{1,0:T(8,128)S(1)}, f32[936,128]{1,0:T(8,128)S(1)}, u32[]{:S(2)}, u32[]{:S(2)}) collective-permute-start(f32[936,128]{1,0:T(8,128)S(1)} %pack0.1), channel_id=1, source_target_pairs={{2,0},{4,2},{6,4},{8,6},{10,8},{12,10},{14,12},{3,1},{5,3},{7,5},{... | collective-permute-start | bytes 1437704 | tf_op jit(solution)/shard_map/ppermute | solution.py:304
  5.9 32.7 %collective-permute-start.3 = (f32[936,128]{1,0:T(8,128)S(1)}, f32[936,128]{1,0:T(8,128)S(1)}, u32[]{:S(2)}, u32[]{:S(2)}) collective-permute-start(f32[936,128]{1,0:T(8,128)S(1)} %pack1.1), channel_id=1, source_target_pairs={{2,0},{4,2},{6,4},{8,6},{10,8},{12,10},{14,12},{3,1},{5,3},{7,5},{... | collective-permute-start | bytes 1437704 | tf_op jit(solution)/shard_map/ppermute | solution.py:304
  7.2 2.2 %copy-start = (s32[4,64,4096]{2,1,0:T(8,128)S(1)}, s32[4,64,4096]{2,1,0:T(8,128)}, u32[]{:S(2)}) copy-start(s32[4,64,4096]{2,1,0:T(8,128)} %index_map.3) | copy-start | bytes 12582916
  9.4 0.7 %copy-start.8 = (s32[5]{0:T(128)S(1)}, s32[5]{0:T(128)}, u32[]{:S(2)}) copy-start(s32[5]{0:T(128)} %period_seq.3) | copy-start | bytes 64
  10.1 0.7 %copy-start.10 = (f32[4]{0:T(128)S(1)}, f32[4]{0:T(128)}, u32[]{:S(2)}) copy-start(f32[4]{0:T(128)} %eps.3) | copy-start | bytes 52
  12.2 13.6 %copy-start.12 = (s32[4]{0:T(128)S(1)}, s32[4]{0:T(128)}, u32[]{:S(2)}) copy-start(s32[4]{0:T(128)} %shifts.3) | copy-start | bytes 52
  12.2 13.6 %collective-permute-start = (f32[152,128]{1,0:T(8,128)}, f32[152,128]{1,0:T(8,128)}, u32[]{:S(2)}, u32[]{:S(2)}) collective-permute-start(f32[152,128]{1,0:T(8,128)} %edge.1), channel_id=1, source_target_pairs={{0,1},{1,0},{2,3},{3,2},{4,5},{5,4},{6,7},{7,6},{8,9},{9,8},{10,11... | collective-permute-start | bytes 233480 | tf_op jit(solution)/shard_map/ppermute | solution.py:314
  21.0 4.8 %collective-permute-start.2 = (f32[64,128]{1,0:T(8,128)S(1)}, f32[64,128]{1,0:T(8,128)S(1)}, u32[]{:S(2)}, u32[]{:S(2)}) collective-permute-start(f32[64,128]{1,0:T(8,128)S(1)} %constant_dynamic-slice_fusion), channel_id=1, source_target_pairs={{0,1},{1,0},{2,3},{3,2},{4,5},{5,4},{6,7},{7,6},{8,9},{9,8},{10,11... | collective-permute-start | bytes 98312 | tf_op jit(solution)/shard_map/ppermute | solution.py:324
  21.1 2.2 %copy-start.1 = (s32[4,64,4096]{2,1,0:T(8,128)S(1)}, s32[4,64,4096]{2,1,0:T(8,128)}, u32[]{:S(2)}) copy-start(s32[4,64,4096]{2,1,0:T(8,128)} %index_map.3) | copy-start | bytes 12582916

commit v2 on v1

v2 whole, which is shorter than its diff:
```python
import functools

import jax
import jax.numpy as jnp
from jax import lax
from jax.experimental import pallas as pl
from jax.experimental.pallas import tpu as pltpu
from jax.sharding import PartitionSpec as P

ITERS = 4
SMAX = 4
LANES = 128
TILE = 8
OUTER = 16
AHEAD = 4
BOUNDS = tuple(range(SMAX + 2, ITERS * SMAX + 1, 2))

courant = 0.6

VMEM = pltpu.VMEM
HBM = pltpu.HBM


def up(value, unit):
    return -(-value // unit) * unit


def spec(space):
    return pl.BlockSpec(memory_space=space)


def pack_kernel(
    plan, bounds, period_seq, eps, shifts, e, hx, hz, index_map, inner_out, outer_out, which_out,
    buf, levels, coeff, *scratch,
):
    work, sem = scratch[:-1], scratch[-1]
    low = lax.axis_index("gz") == 0
    strips, head = plan.strips, buf.shape[1]
    groups = head // TILE
    copies = [pltpu.make_async_copy(field.at[pl.ds(0, head), :], buf.at[i], sem.at[i]) for i, field in enumerate((e, hx, hz))]
    for group in range(groups):
        copies.append(
            pltpu.make_async_copy(
                map_rows(plan, period_seq, index_map, group, 0, strips * LANES),
                levels.at[pl.ds(group * TILE, TILE), :],
                sem.at[3 + group],
            )
        )
    for copy in copies:
        copy.start()
    total = way(shifts)
    which = jnp.int32(0)
    bound = jnp.int32(bounds[0])
    for now, after in zip(bounds[:-1], bounds[1:]):
        which = which + (total > now).astype(jnp.int32)
        bound = bound + jnp.where(total > now, after - now, 0)
    which_out[0] = which
    base = jnp.maximum(total - ITERS, 0)
    inverse = inverse_table(eps)
    for copy in copies:
        copy.wait()

    fields, source = work[0:3], work[3:6]
    for strip in range(strips):
        lanes = pl.ds(strip * LANES, LANES)
        for i in range(3):
            source[i][strip] = buf[i, :, lanes]
        source_levels = work[6]
        source_levels[strip] = levels[:, lanes]
    sets = [fields] + [work[7 + 4 * k : 11 + 4 * k] for k in range(ITERS - 1)]

    def read(step, i, strip):
        if step == 0:
            return source[i][strip, pl.ds(base, TILE), :]
        return sets[step][i][strip]

    def factor(step, strip):
        if step == 0:
            coeff[strip] = material_of(work[6][strip, pl.ds(base, TILE), :], inverse)
        return coeff[strip]

    def write(step, strip, *values):
        for ref, value in zip(sets[step + 1], values):
            ref[strip] = value

    march(ITERS - 1, strips, TILE, read, factor, write)

    sent = 3 * bound + ITERS
    place = (0, bound + 1, 2 * bound + 1, 3 * bound + 1)

    def put(out, at, strip):
        for i in range(3):
            for q in range(groups):
                out[pl.ds(at + place[i] + q * TILE, TILE), :] = source[i][strip, pl.ds(q * TILE, TILE), :]
        for step in range(1, ITERS):
            out[pl.ds(at + place[3] + step - 1, 1), :] = sets[step][0][strip, pl.ds(ITERS, 1), :]

    inner, outer = plan.count
    for k in range(inner):
        put(inner_out, k * sent, jnp.where(low, outer + k, inner - 1 - k))
    for i in range(3):
        side = jnp.where(low, strips - 1, 0)
        inner_out[pl.ds(inner * sent + i * TILE, TILE), :] = source[i][side, pl.ds(bound, TILE), :]
    for k in range(outer):
        put(outer_out, k * sent, jnp.where(low, k, inner + k))


def way(shifts):
    total = shifts[0]
    for step in range(1, ITERS):
        total = total + shifts[step]
    return total


def march(steps, strips, used, read, factor, write, mask=None):
    lane = lax.broadcasted_iota(jnp.int32, (used, LANES), 1)
    last_lane, first_lane = lane == LANES - 1, lane == 0
    none = jnp.zeros((used, LANES), jnp.float32)
    for step in range(steps):
        above, below = mask(step) if mask else (None, None)
        values, left, right, hx_right = {}, {strips: none}, {-1: none}, {-1: none}
        for strip in range(-AHEAD, strips):
            coming = strip + AHEAD
            if coming < strips:
                values[coming] = read(step, 0, coming)
                left[coming] = pltpu.roll(values[coming], LANES - 1, 1)
                right[coming] = pltpu.roll(values[coming], 1, 1)
                if step == 0:
                    hx_right[coming] = pltpu.roll(read(step, 1, coming), 1, 1)
            if strip < 0:
                continue
            field_e = values.pop(strip)
            upper = jnp.where(last_lane, left[strip + 1], left[strip])
            under = jnp.where(first_lane, right[strip - 1], right[strip])
            if step == 0:
                lower = jnp.where(first_lane, hx_right[strip - 1], hx_right[strip])
            else:
                lower = read(step, 3, strip)
            field_hx = read(step, 1, strip) + courant * (upper - field_e)
            lower = lower + courant * (field_e - under)
            if strip == 0:
                lower = jnp.where(first_lane, 0.0, lower)
            ahead = pltpu.roll(field_e, used - 1, 0)
            field_hz = read(step, 2, strip) - courant * (ahead - field_e)
            if above is not None:
                field_hz = jnp.where(above, field_hz, 0.0)
            behind = pltpu.roll(field_hz, 1, 0)
            moved = field_e + factor(step, strip) * ((field_hx - lower) - (field_hz - behind))
            if below is not None:
                moved = jnp.where(below, moved, 0.0)
            write(step, strip, moved, field_hx, field_hz, lower)


def material_of(levels, inverse):
    result = jnp.zeros(levels.shape, jnp.float32)
    for level, value in enumerate(inverse):
        result = jnp.where(levels == level, value, result)
    return result


def inverse_table(eps):
    return [courant * (1.0 / jnp.full((TILE, LANES), eps[i], jnp.float32)) for i in range(eps.shape[0])]


def map_rows(plan, period_seq, index_map, group, first, width):
    span = index_map.shape[1]
    cell = lax.axis_index("gx") * plan.rows + group * TILE
    period = jnp.minimum(cell // span, period_seq.shape[0] - 1)
    phase = pl.multiple_of(cell % span, TILE)
    return index_map.at[period_seq[period], pl.ds(phase, TILE), pl.ds(first, width)]


def prepare_kernel(
    plan, period_seq, eps, e, hx, hz, index_map, edge, e_out, hx_out, hz_out, coeff,
    levels, edge_sem, field_sem, sem,
):
    low = lax.axis_index("gz") == 0
    first = pl.multiple_of(jnp.where(low, plan.strips - 1, 0) * LANES, LANES)
    rows, strips = plan.rows, plan.strips
    groups = plan.reach // TILE
    fields = (e, hx, hz)
    edges = [
        pltpu.make_async_copy(
            field.at[:, pl.ds(first, LANES)], edge.at[pl.ds(i * rows, rows), :], edge_sem.at[i]
        )
        for i, field in enumerate(fields)
    ]
    maps = [
        pltpu.make_async_copy(
            map_rows(plan, period_seq, index_map, group, 0, strips * LANES),
            levels.at[pl.ds(group * TILE, TILE), :],
            sem.at[group],
        )
        for group in range(groups)
    ]
    for copy in edges + maps:
        copy.start()

    def field_copy(i, strip):
        return pltpu.make_async_copy(
            fields[i].at[:, pl.ds(pl.multiple_of(strip * LANES, LANES), LANES)],
            (e_out, hx_out, hz_out)[i].at[strip, pl.ds(0, rows), :],
            field_sem.at[i, strip],
        )

    def start_strip(strip, _):
        for i in range(3):
            field_copy(i, strip).start()
        return 0

    lax.fori_loop(0, strips, start_strip, 0)
    inverse = inverse_table(eps)
    for copy in maps:
        copy.wait()

    def strip_of(strip, _):
        lanes = pl.ds(pl.multiple_of(strip * LANES, LANES), LANES)
        for group in range(groups):
            at = pl.ds(group * TILE, TILE)
            coeff[strip, at, :] = material_of(levels[at, lanes], inverse)
        return 0

    lax.fori_loop(0, strips, strip_of, 0, unroll=2)
    for group in range(groups):
        at = pl.ds(group * TILE, TILE)
        edge[pl.ds(3 * rows + group * TILE, TILE), :] = material_of(levels[at, pl.ds(first, LANES)], inverse)
    for copy in edges:
        copy.wait()

    def wait_strip(strip, _):
        for i in range(3):
            field_copy(i, strip).wait()
        return 0

    lax.fori_loop(0, strips, wait_strip, 0)


def update_kernel(plan, part, shifts, *refs):
    fields, coeff, halo, halo_lead, leads = refs[0:3], refs[3], refs[4], refs[5], refs[6 : 7 + part]
    refs = refs[7 + part :]
    if part:
        refs = refs[3:]
    outs, source, source_coeff, source_behind = refs[0:3], refs[3:6], refs[6], refs[7]
    work, work_coeff, stage, sem = refs[8:16], refs[16], refs[17], refs[18]
    low = lax.axis_index("gz") == 0
    rows, reach, used = plan.rows, plan.reach, plan.used
    lead_rows = reach - rows
    local = plan.local[part]

    def own(strip, to):
        for i in range(3):
            source[i][to, pl.ds(0, rows), :] = fields[i][strip, pl.ds(0, rows), :]
        source_coeff[to] = coeff[strip]

    def lead(sent, at, to):
        for i in range(3):
            for q in range(lead_rows // TILE):
                source[i][to, pl.ds(rows + q * TILE, TILE), :] = sent[pl.ds(at + plan.place[i] + q * TILE, TILE), :]
        source_behind[to] = sent[pl.ds(at + plan.place[3], TILE), :]

    def lead_side(sent, at, to):
        for i in range(3):
            source[i][to, pl.ds(rows + plan.moved, TILE), :] = sent[pl.ds(at + i * TILE, TILE), :]

    inner, outer = plan.count
    if part == 0:
        for k in range(inner):
            strip = jnp.where(low, outer + k, inner - 1 - k)
            to = jnp.where(low, k, inner - k)
            own(strip, to)
            lead(leads[0], k * plan.sent, to)
        lead_side(leads[0], inner * plan.sent, jnp.where(low, inner - 1, 1))
        side = jnp.where(low, inner, 0)
        for i in range(3):
            source[i][side, pl.ds(0, rows), :] = halo[pl.ds(i * rows, rows), :]
        source_coeff[side] = halo[pl.ds(3 * rows, reach), :]
        lead(halo_lead, plan.side, side)
        lead_side(halo_lead, plan.side + plan.sent, side)
        done, kept = 1, inner - 1
        column = jnp.where(low, outer + 1, 0)
    else:
        for k in range(outer):
            to = jnp.where(low, k, k + 2)
            own(jnp.where(low, k, inner + k), to)
            lead(leads[1], k * plan.sent, to)
        for k in range(2):
            to = jnp.where(low, outer + k, 1 - k)
            own(jnp.where(low, outer + k, inner - 1 - k), to)
            lead(leads[0], k * plan.sent, to)
        done, kept = jnp.where(low, 0, 1), outer + 1
        column = jnp.where(low, 0, inner - 1)

    row = lax.broadcasted_iota(jnp.int32, (used, LANES), 0)
    total = lax.axis_size("gx") * rows
    base = jnp.maximum(way(shifts) - ITERS, 0)
    start = lax.axis_index("gx") * rows + base
    sets = (work[0:4], work[4:8])
    lane = lax.broadcasted_iota(jnp.int32, (1, LANES), 1)
    half = LANES // 2
    known = {}
    if part == 0:
        known[0] = (0, LANES), (LANES, LANES)
        known[1] = (0, LANES), (half, LANES)
        known[inner - 1] = (0, half), (0, LANES)
        known[inner] = (0, 0), (0, LANES)

    def mask(step):
        offset = shifts[0]
        for earlier in range(step):
            offset = offset + shifts[earlier + 1]
        return row >= offset - start, row < offset + total - start

    def read(step, i, strip):
        if step == 0:
            return source[i][strip, pl.ds(base, used), :]
        return sets[step % 2][i][strip]

    def factor(step, strip):
        if step == 0:
            work_coeff[strip] = source_coeff[strip, pl.ds(base, used), :]
        return work_coeff[strip]

    def write(step, strip, *values):
        later = sets[(step + 1) % 2]
        for ref, value in zip(later, values):
            ref[strip] = value
        if step + 1 < ITERS:
            behind = source_behind[strip, pl.ds(step, 1), :]
            at = pl.ds(rows + ITERS, 1)
            if strip in known:
                lows, highs = known[strip]
                inside = (lane >= jnp.where(low, lows[0], highs[0])) & (lane < jnp.where(low, lows[1], highs[1]))
                behind = jnp.where(inside, behind, values[0][rows + ITERS : rows + ITERS + 1])
            later[0][strip, at, :] = behind

    march(ITERS, local, used, read, factor, write, mask)
    for k in range(kept):
        lanes = pl.ds(k * LANES, LANES)
        for i, ref in enumerate(sets[ITERS % 2][0:3]):
            stage[i, :, lanes] = ref[done + k, pl.ds(ITERS, rows), :]
    column = pl.multiple_of(column * LANES, LANES)
    copies = [
        pltpu.make_async_copy(stage.at[i], outs[i].at[:, pl.ds(column, kept * LANES)], sem.at[i])
        for i in range(3)
    ]
    for copy in copies:
        copy.start()
    for copy in copies:
        copy.wait()


class Plan:
    def __init__(self, rows, cols, moved):
        assert rows % TILE == 0 and cols % LANES == 0
        self.rows = rows
        self.strips = cols // LANES
        self.reach = up(rows + ITERS * SMAX + ITERS, TILE)
        self.used = up(rows + 2 * ITERS, TILE)
        self.head = self.reach - rows
        assert rows >= self.head and self.used <= self.reach
        self.count = (self.strips - OUTER, OUTER)
        self.local = (self.count[0] + 1, OUTER + 2)
        self.moved = moved
        self.place = (0, moved + 1, 2 * moved + 1, 3 * moved + 1)
        self.sent = 3 * moved + ITERS
        first = (self.count[0] - 1) * self.sent
        self.cut = first // TILE * TILE
        self.side = first - self.cut

    def buffer(self, part):
        behind = max(self.place[2] + self.head, self.place[3] + TILE)
        end = (self.count[part] - 1) * self.sent + behind
        return up(max(end, self.count[part] * self.sent + 3 * TILE), TILE)


def call(kernel, name, outs, ins, out_spaces, scratch, aliases=None, flops=1 << 20):
    return pl.pallas_call(
        kernel,
        name=name,
        out_shape=outs,
        in_specs=[spec(space) for space in ins],
        out_specs=[spec(space) for space in out_spaces],
        scratch_shapes=scratch,
        input_output_aliases=aliases or {},
        cost_estimate=pl.CostEstimate(flops=flops, bytes_accessed=flops, transcendentals=0),
        compiler_params=pltpu.CompilerParams(vmem_limit_bytes=16 << 20),
    )


def f32(*shape):
    return VMEM(shape, jnp.float32)


def advance(moved, inner_sent, outer_sent, electric, magnetic_x, magnetic_z, index_map, period_seq, eps_table, shifts):
    rows, cols = electric.shape
    plan = Plan(rows, cols, moved)
    strips, reach = plan.strips, plan.reach
    fields = (electric, magnetic_x, magnetic_z)
    count_x = lax.axis_size("gx")
    back = [(i + 1, i) for i in range(count_x - 1)]
    swap = [(0, 1), (1, 0)]
    leads = [
        lax.ppermute(lax.slice_in_dim(packed, 0, plan.buffer(part), axis=0), "gx", back)
        for part, packed in enumerate((inner_sent, outer_sent))
    ]
    groups = reach // TILE
    edge, *held, coeff = call(
        functools.partial(prepare_kernel, plan),
        "prepare",
        [f32(3 * rows + reach, LANES)] + [f32(strips, reach, LANES)] * 4,
        [pltpu.SMEM] * 2 + [HBM] * 4,
        [VMEM] * 5,
        [
            VMEM((reach, cols), jnp.int32),
            pltpu.SemaphoreType.DMA((3,)),
            pltpu.SemaphoreType.DMA((3, strips)),
            pltpu.SemaphoreType.DMA((groups,)),
        ],
    )(period_seq, eps_table, *fields, index_map)
    halo = lax.ppermute(edge, "gz", swap)
    halo_lead = lax.ppermute(lax.slice_in_dim(leads[0], plan.cut, None, axis=0), "gz", swap)
    outs = ()
    for part in range(2):
        kept = (plan.count[0] - 1, plan.count[1] + 1)[part]
        local = plan.local[part]
        work = [VMEM((local, reach, LANES), jnp.float32)] * 4 + [VMEM((local, TILE, LANES), jnp.float32)]
        work += [VMEM((local, plan.used, LANES), jnp.float32)] * 9
        outs = call(
            functools.partial(update_kernel, plan, part),
            f"update{part}",
            [HBM((rows, cols), jnp.float32)] * 3,
            [pltpu.SMEM] + [VMEM] * (7 + part) + [HBM] * len(outs),
            [HBM] * 3,
            work + [VMEM((3, rows, kept * LANES), jnp.float32), pltpu.SemaphoreType.DMA((3,))],
            {8 + part + i: i for i in range(len(outs))},
        )(shifts, *held, coeff, halo, halo_lead, *leads[: 1 + part], *outs)
    return tuple(outs)


def body(electric, magnetic_x, magnetic_z, index_map, period_seq, eps_table, shifts):
    rows, cols = electric.shape
    electric, magnetic_x, magnetic_z, index_map = (
        pltpu.with_memory_space_constraint(item, HBM) for item in (electric, magnetic_x, magnetic_z, index_map)
    )
    rest = (electric, magnetic_x, magnetic_z, index_map, period_seq, eps_table, shifts)
    plan = Plan(rows, cols, BOUNDS[-1])
    strips, head = plan.strips, plan.head
    inner_sent, outer_sent, which = call(
        functools.partial(pack_kernel, plan, BOUNDS),
        "pack",
        [f32(plan.buffer(0), LANES), f32(plan.buffer(1), LANES), pltpu.SMEM((1,), jnp.int32)],
        [pltpu.SMEM] * 3 + [HBM] * 4,
        [VMEM, VMEM, pltpu.SMEM],
        [
            VMEM((3, head, cols), jnp.float32),
            VMEM((head, cols), jnp.int32),
            VMEM((strips, TILE, LANES), jnp.float32),
        ]
        + [VMEM((strips, TILE, LANES), jnp.float32)] * 3
        + [VMEM((strips, head, LANES), jnp.float32)] * 3
        + [VMEM((strips, head, LANES), jnp.int32)]
        + [VMEM((strips, TILE, LANES), jnp.float32)] * (4 * (ITERS - 1))
        + [pltpu.SemaphoreType.DMA((3 + head // TILE,))],
    )(period_seq, eps_table, shifts, electric, magnetic_x, magnetic_z, index_map)
    return lax.switch(which[0], [functools.partial(advance, bound) for bound in BOUNDS], inner_sent, outer_sent, *rest)


def solution(mesh):
    assert mesh.shape["gz"] == 2
    placed = (
        P(("grp", "gx"), "gz"),
        P(("grp", "gx"), "gz"),
        P(("grp", "gx"), "gz"),
        P(None, None, "gz"),
        P("grp"),
        P(),
        P("grp"),
    )
    return jax.shard_map(
        body,
        mesh=mesh,
        in_specs=placed,
        out_specs=(P(("grp", "gx"), "gz"), P(("grp", "gx"), "gz"), P(("grp", "gx"), "gz")),
        check_vma=False,
    )
```

time: 53.3 us -> 27.3 us (0.51); the launches traced: 52.3 us -> 27.1 us
  Pallas kernels: 31 us -> 12.1 us
  local copies, waits for them, and re-layouts: 8.84 us -> 0.06 us
  waiting for transfers between devices: 8.25 us -> 10.6 us
    pallas_call x6 -> x4, Pallas kernels: 31 us -> 12.1 us  [the longest x2 5.94 us: advance(): call(functools.partial(update_kernel, plan, part), f'update{part}', [HBM(...]
    unnamed x26 -> x6, local copies, waits for them, and re-layouts: 8.83 us -> 0.01 us
    ppermute x3, waiting for transfers between devices: 8.24 us -> 10.6 us  [the longest x2 9.41 us: advance(): lax.ppermute(lax.slice_in_dim(packed, 0, plan.buffer(part), axis=0), 'gx'...]
  transfers between devices with their start and end apart: 4 -> 4, of which waited for: 1 -> 3; matrix products, arithmetic and copies ran while one was open for 0% -> 0% of each run, Pallas kernels for 33% -> 23%
where the time goes in v2:
time: 27.3 us; the launch traced here: 27.1 us
  Pallas kernels  12.1 us (44%)
  waiting for transfers between devices  10.6 us (39%)
  starting transfers between devices  3.14 us (12%)
  between operations  0.87 us (3%)
  loops' own time  0.31 us (1%)
    ppermute x2, waiting for transfers between devices, advance(): lax.ppermute(lax.slice_in_dim(packed, 0, plan.buffer(part), axis=0), 'gx'...  9.41 us
    pallas_call x2, Pallas kernels, advance(): call(functools.partial(update_kernel, plan, part), f'update{part}', [HBM(...  5.94 us
    pallas_call x1, Pallas kernels, advance(): call(functools.partial(prepare_kernel, plan), 'prepare', [f32(3 * rows +...  3.4 us
    pallas_call x1, Pallas kernels, body(): call(functools.partial(pack_kernel, plan, BOUNDS), 'pack', [f32(plan.buff...  2.78 us
    ppermute x2, starting transfers between devices, advance(): lax.ppermute(lax.slice_in_dim(packed, 0, plan.buffer(part), axis=0), 'gx'...  2.58 us
    ppermute x1, waiting for transfers between devices, advance(): lax.ppermute(lax.slice_in_dim(leads[0], plan.cut, None, axis=0), 'gz', swap)  1.2 us
    ppermute x1, starting transfers between devices, advance(): halo = lax.ppermute(edge, 'gz', swap)  0.55 us
  transfers between devices with their start and end apart: 4, of which 3 were waited for; matrix products, arithmetic and copies ran while one was open for 0% of the time, Pallas kernels for 23%

profile of v2, /device:TPU:0, one launch (start us, length us, event | category | flops | bytes accessed | tf_op | source)
XLA Modules:
  0.0 27.1 jit_solution(5651731821662397156)
XLA Ops:
  0.6 0.0 copy-start
  0.6 0.0 copy-start.2
  0.7 0.0 copy-start.1
  0.7 2.8 %pack.1 = (f32[856,128]{1,0:T(8,128)S(1)}, f32[856,128]{1,0:T(8,128)S(1)}, s32[1]{0:T(128)S(4)}) custom-call(s32[5]{0:T(128)} %period_seq.1, f32[4]{0:T(128)} %eps.1, s32[4]{0:T(128)} %shifts.1, f32[32,4096]{1,0:T(8,128)} %e.1, f32[32,4096]{1,0:T(8,128)} %hx.1, f32[32,4096]{1,0:T(8,128)} %hz.1, s32[4,64,4096]{2,1,0:T(8,128)} %index_map.1), custom_call_target="tpu_custom_call" | custom-call | flops 1048576 | bytes 1048576 | tf_op jit(solution)/shard_map/pack/pallas_call | solution.py:448
  3.5 0.0 copy-done
  3.5 0.0 copy-done.2
  3.5 0.0 copy-done.1
  3.5 23.5 %conditional.1 = ((f32[32,4096]{1,0:T(8,128)}, f32[32,4096]{1,0:T(8,128)}, f32[32,4096]{1,0:T(8,128)})) conditional(s32[]{:T(128)} %bitcast, (s32[5]{0:T(128)S(1)}, f32[4]{0:T(128)S(1)}, f32[32,4096]{1,0:T(8,128)}, f32[32,4096]{1,0:T(8,128)}, f32[32,4096]{1,0:T(8,128)}, /*index=5*/s32[4,64,4096]{2,1,0:T(8,128)}, ...), branch_computations={%region_0.0_spmd, %region_1.0_spmd, %region_2.0_spmd, %region_3.0_... | conditional | flops 3145728 | bytes 8347816 | solution.py:465
  3.8 1.3 %collective-permute-start.13 = (f32[664,128]{1,0:T(8,128)S(1)}, f32[664,128]{1,0:T(8,128)S(1)}, u32[]{:S(2)}, u32[]{:S(2)}) collective-permute-start(f32[664,128]{1,0:T(8,128)S(1)} %slice.41), channel_id=1, source_target_pairs={{2,0},{4,2},{6,4},{8,6},{10,8},{12,10},{14,12},{3,1},{5,3},{7,5},{... | collective-permute-start | bytes 1019912 | tf_op jit(solution)/shard_map/cond/branch_3_fun/ppermute | solution.py:403
  5.1 1.3 %collective-permute-start.15 = (f32[664,128]{1,0:T(8,128)S(1)}, f32[664,128]{1,0:T(8,128)S(1)}, u32[]{:S(2)}, u32[]{:S(2)}) collective-permute-start(f32[664,128]{1,0:T(8,128)S(1)} %slice.43), channel_id=1, source_target_pairs={{2,0},{4,2},{6,4},{8,6},{10,8},{12,10},{14,12},{3,1},{5,3},{7,5},{... | collective-permute-start | bytes 1019912 | tf_op jit(solution)/shard_map/cond/branch_3_fun/ppermute | solution.py:403
  6.4 3.4 %prepare.9 = (f32[152,128]{1,0:T(8,128)S(1)}, f32[32,56,128]{2,1,0:T(8,128)S(1)}, f32[32,56,128]{2,1,0:T(8,128)S(1)}, f32[32,56,128]{2,1,0:T(8,128)S(1)}, f32[32,56,128]{2,1,0:T(8,128)S(1)}) custom-call(s32[5]{0:T(128)S(1)} %get-tuple-element.160.period_seq, f32[4]{0:T(128)S(1)} %get-tuple-element.161.eps, f32[32,4096]{1,0:T(8,128)} %get-tuple-element.162.e, ...), custom_call_target="tpu_custom_call" | custom-call | flops 1048576 | bytes 1048576 | tf_op jit(solution)/shard_map/cond/branch_3_fun/prepare/pallas_call | solution.py:407
  9.8 0.6 %collective-permute-start.12 = (f32[152,128]{1,0:T(8,128)S(1)}, f32[152,128]{1,0:T(8,128)S(1)}, u32[]{:S(2)}, u32[]{:S(2)}) collective-permute-start(f32[152,128]{1,0:T(8,128)S(1)} %get-tuple-element.170), channel_id=1, source_target_pairs={{0,1},{1,0},{2,3},{3,2},{4,5},{5,4},{6,7},{7,6},{8,9},{9,8},{10,11... | collective-permute-start | bytes 233480 | tf_op jit(solution)/shard_map/cond/branch_3_fun/ppermute | solution.py:420
  10.4 7.1 %collective-permute-done.13.refs_6_ = f32[664,128]{1,0:T(8,128)S(1)} collective-permute-done((f32[664,128]{1,0:T(8,128)S(1)}, f32[664,128]{1,0:T(8,128)S(1)}, u32[]{:S(2)}, u32[]{:S(2)}) %collective-permute-start.13) | collective-permute-done | bytes 340000 | tf_op jit(solution)/shard_map/cond/branch_3_fun/ppermute | solution.py:403
  17.5 0.0 collective-permute-start.14
  17.5 0.0 collective-permute-done.12.refs_4_
  17.5 1.2 %collective-permute-done.14.refs_5_ = f32[64,128]{1,0:T(8,128)S(1)} collective-permute-done((f32[64,128]{1,0:T(8,128)S(1)}, f32[64,128]{1,0:T(8,128)S(1)}, u32[]{:S(2)}, u32[]{:S(2)}) %collective-permute-start.14) | collective-permute-done | bytes 32800 | tf_op jit(solution)/shard_map/cond/branch_3_fun/ppermute | solution.py:421
  18.7 2.9 %update0.9 = (f32[32,4096]{1,0:T(8,128)}, f32[32,4096]{1,0:T(8,128)}, f32[32,4096]{1,0:T(8,128)}) custom-call(s32[4]{0:T(128)S(1)} %get-tuple-element.159.shifts, f32[32,56,128]{2,1,0:T(8,128)S(1)} %get-tuple-element.166.refs_0_, f32[32,56,128]{2,1,0:T(8,128)S(1)} %get-tuple-element.167.refs_1_, f32[32,56,128]{2,1,0:T(8,128)S(1)} %get-tuple-element.168.refs_2_, ...), custom_call_target="tpu_custom_call" | custom-call | flops 1048576 | bytes 1048576 | tf_op jit(solution)/shard_map/cond/branch_3_fun/update0/pallas_call | solution.py:428
  21.6 2.3 %collective-permute-done.15.refs_7_ = f32[664,128]{1,0:T(8,128)S(1)} collective-permute-done((f32[664,128]{1,0:T(8,128)S(1)}, f32[664,128]{1,0:T(8,128)S(1)}, u32[]{:S(2)}, u32[]{:S(2)}) %collective-permute-start.15) | collective-permute-done | bytes 340000 | tf_op jit(solution)/shard_map/cond/branch_3_fun/ppermute | solution.py:403
  23.9 3.0 %update1.9 = (f32[32,4096]{1,0:T(8,128)}, f32[32,4096]{1,0:T(8,128)}, f32[32,4096]{1,0:T(8,128)}) custom-call(s32[4]{0:T(128)S(1)} %get-tuple-element.159.shifts, f32[32,56,128]{2,1,0:T(8,128)S(1)} %get-tuple-element.166.refs_0_, f32[32,56,128]{2,1,0:T(8,128)S(1)} %get-tuple-element.167.refs_1_, ...), custom_call_target="tpu_custom_call", output_to_operand_aliasing={{0}: (9, {}), {1}: (10, {}), {2}: (11, {})} | custom-call | flops 1048576 | bytes 1048576 | tf_op jit(solution)/shard_map/cond/branch_3_fun/update1/pallas_call | solution.py:428
  (3 shorter events, 0.1 us)
Async XLA Ops:
  0.6 2.8 %copy-start = (s32[4]{0:T(128)S(1)}, s32[4]{0:T(128)}, u32[]{:S(2)}) copy-start(s32[4]{0:T(128)} %shifts.1) | copy-start | bytes 52
  0.6 2.8 %copy-start.2 = (f32[4]{0:T(128)S(1)}, f32[4]{0:T(128)}, u32[]{:S(2)}) copy-start(f32[4]{0:T(128)} %eps.1) | copy-start | bytes 52
  0.7 2.8 %copy-start.1 = (s32[5]{0:T(128)S(1)}, s32[5]{0:T(128)}, u32[]{:S(2)}) copy-start(s32[5]{0:T(128)} %period_seq.1) | copy-start | bytes 64
  3.8 13.7 %collective-permute-start.13 = (f32[664,128]{1,0:T(8,128)S(1)}, f32[664,128]{1,0:T(8,128)S(1)}, u32[]{:S(2)}, u32[]{:S(2)}) collective-permute-start(f32[664,128]{1,0:T(8,128)S(1)} %slice.41), channel_id=1, source_target_pairs={{2,0},{4,2},{6,4},{8,6},{10,8},{12,10},{14,12},{3,1},{5,3},{7,5},{... | collective-permute-start | bytes 1019912 | tf_op jit(solution)/shard_map/cond/branch_3_fun/ppermute | solution.py:403
  5.1 18.8 %collective-permute-start.15 = (f32[664,128]{1,0:T(8,128)S(1)}, f32[664,128]{1,0:T(8,128)S(1)}, u32[]{:S(2)}, u32[]{:S(2)}) collective-permute-start(f32[664,128]{1,0:T(8,128)S(1)} %slice.43), channel_id=1, source_target_pairs={{2,0},{4,2},{6,4},{8,6},{10,8},{12,10},{14,12},{3,1},{5,3},{7,5},{... | collective-permute-start | bytes 1019912 | tf_op jit(solution)/shard_map/cond/branch_3_fun/ppermute | solution.py:403
  9.8 7.7 %collective-permute-start.12 = (f32[152,128]{1,0:T(8,128)S(1)}, f32[152,128]{1,0:T(8,128)S(1)}, u32[]{:S(2)}, u32[]{:S(2)}) collective-permute-start(f32[152,128]{1,0:T(8,128)S(1)} %get-tuple-element.170), channel_id=1, source_target_pairs={{0,1},{1,0},{2,3},{3,2},{4,5},{5,4},{6,7},{7,6},{8,9},{9,8},{10,11... | collective-permute-start | bytes 233480 | tf_op jit(solution)/shard_map/cond/branch_3_fun/ppermute | solution.py:420
  17.5 1.2 %collective-permute-start.14 = (f32[64,128]{1,0:T(8,128)S(1)}, f32[64,128]{1,0:T(8,128)S(1)}, u32[]{:S(2)}, u32[]{:S(2)}) collective-permute-start(f32[64,128]{1,0:T(8,128)S(1)} %slice.51), channel_id=1, source_target_pairs={{0,1},{1,0},{2,3},{3,2},{4,5},{5,4},{6,7},{7,6},{8,9},{9,8},{10,11... | collective-permute-start | bytes 98312 | tf_op jit(solution)/shard_map/cond/branch_3_fun/ppermute | solution.py:421
